TPU v7x, 32 devices: a whole 2x2x4 slice. The times are simulated.
32 devices in a mesh: samp: 8 (over z, y), snp: 4 (over x, core).
Axes of the slice: x: 2, y: 2, z: 4, core: 2. Of those that a mesh axis runs over, the one named last changes fastest.
Arguments:
- geno_words: int32 [2048, 1024], P('samp', 'snp'), may hold values from -2147483648 to 2147483647, as said below
- counts: int32 [2048], P('samp'), may hold values from 0 to 4, as said below
- probes: bfloat16 [2048, 64], P('samp'), may hold values from -6 to 6
- phenotype: float32 [2048], P('samp'), may hold values from -6 to 6
- tile_comp: int32 [128], replicated, may hold values from 0 to 7, as said below
Outputs:
- images: bfloat16 [2048, 512], P(('samp', 'snp'))
- traces: float32 [8, 8], replicated
- yky: float32 [8], replicated
Inputs may be any that keep to these rules, and one draw needn't show every extreme that they name: `geno_words`: each word packs sixteen dosages of one sample in 2-bit fields as step one reads them; every field holds 0, 1 or 2. `counts`: at least one sample has a count of one or more. `tile_comp`: every component owns at least one tile.
All inputs are finite; a program needn't handle non-finite values.
Results may differ from a plain program's by a relative error of at most 0.015.
Values may be sent and summed in bfloat16 or wider, within the bound.
A program may use at most 64 MiB of HBM per device.

v0:
```python
import jax
import jax.numpy as jnp
from jax import lax
from jax.sharding import PartitionSpec as P

SNPS = 16384
COMPS = 8


EPSILON = 1e-05


def unpack_rows(packed):
    height = packed.shape[0]
    grouped = packed.reshape(height, -1, 1, 128)
    shifts = 2 * jnp.arange(16, dtype=jnp.int32).reshape(1, 1, 16, 1)
    fields = jnp.right_shift(grouped, shifts) & 3
    return fields.reshape(height, -1).astype(jnp.bfloat16)


def block_number(row_count):
    number = 1
    while row_count // number > 768 or row_count % number != 0:
        number = number + 1
    return number


def finish(panel_part, moment_part, totals, inverse, member):
    weight_total = totals[0]
    pheno_total = totals[1]
    probe_total = totals[2:]
    average = moment_part[0] / weight_total
    second = moment_part[1] / weight_total
    spread = 1.0 / jnp.sqrt(second - average * average + EPSILON)
    unit_panel = spread[:, None] * (panel_part - average[:, None] * probe_total[None, :])
    pheno_unit = spread * (moment_part[2] - average * pheno_total)
    coefficients = (spread[:, None] * unit_panel * inverse[:, None]).astype(jnp.bfloat16)
    energy = jnp.sum(member * (pheno_unit * pheno_unit * inverse)[:, None], axis=0)
    return (average, coefficients, energy)


def on_device(geno_words, counts, probes, phenotype, tile_comp):
    height = geno_words.shape[0]
    snp_local = geno_words.shape[1] * 16
    tile_local = snp_local // 128
    probe_count = probes.shape[1]
    weights = counts.astype(jnp.float32)
    root_weight = jnp.sqrt(weights)
    probe_rows = (probes.astype(jnp.float32) * root_weight[:, None]).astype(jnp.bfloat16)
    pheno_rows = (phenotype * root_weight).astype(jnp.bfloat16)
    count_rows = counts.astype(jnp.bfloat16)
    left_rows = jnp.stack([count_rows, pheno_rows], axis=1)
    dosage = unpack_rows(geno_words)
    cross_panel = jnp.einsum("rj,rb->jb", dosage, probe_rows, preferred_element_type=jnp.float32)
    linear = jnp.einsum("rc,rj->cj", left_rows, dosage, preferred_element_type=jnp.float32)
    squares = jnp.einsum("r,rj->j", count_rows, dosage * dosage, preferred_element_type=jnp.float32)
    moments = jnp.stack([linear[0], squares, linear[1]])
    totals = jnp.concatenate(
        [
            jnp.sum(weights)[None],
            jnp.sum(pheno_rows.astype(jnp.float32))[None],
            jnp.sum(probe_rows.astype(jnp.float32), axis=0),
        ]
    )
    levels = jnp.arange(COMPS, dtype=jnp.int32)
    member_all = (tile_comp[:, None] == levels[None, :]).astype(jnp.float32)
    comp_sizes = 128.0 * jnp.sum(member_all, axis=0)
    member_tiles = lax.dynamic_slice_in_dim(
        member_all, lax.axis_index("snp") * tile_local, tile_local, 0
    )
    member_snps = jnp.repeat(member_tiles, 128, axis=0)
    inverse = jnp.sum(member_snps * (1.0 / comp_sizes)[None, :], axis=1)
    summed_panel, summed_moments, totals = lax.psum(
        (cross_panel.reshape(-1, 128), moments, totals), "samp"
    )
    average, coefficients, energy = finish(
        summed_panel.reshape(snp_local, probe_count), summed_moments, totals, inverse, member_snps
    )
    energy = lax.psum(energy, "snp")
    coef_tiles = coefficients.reshape(tile_local, 128, probe_count)
    centre = jnp.sum(average.reshape(tile_local, 128, 1) * coef_tiles.astype(jnp.float32), axis=1)
    quarter = height // lax.axis_size("snp")
    inner_count = block_number(quarter * lax.axis_size("snp"))
    piece_rows = quarter * lax.axis_size("snp") // inner_count
    dosage = unpack_rows(geno_words)
    dosage = dosage.reshape(piece_rows, tile_local, 128)
    partial_value = (
        jnp.einsum("rtj,tjb->rtb", dosage, coef_tiles, preferred_element_type=jnp.float32)
        - centre[None]
    )
    grouped = jnp.einsum(
        "rtb,tk->rkb", partial_value, member_tiles, precision=lax.Precision.HIGHEST
    )
    scaled = grouped * root_weight[:, None, None]
    pieces = scaled.reshape(piece_rows, COMPS * probe_count)
    own_images = lax.psum_scatter(pieces, "snp", scatter_dimension=0, tiled=True)
    stacked = own_images.reshape(quarter, COMPS, probe_count)
    local_trace = jnp.einsum("rkb,rlb->kl", stacked, stacked, precision=lax.Precision.HIGHEST)
    trace_sum = lax.psum(local_trace, ("samp", "snp"))
    weight_total = totals[0]
    traces = trace_sum * (SNPS / (COMPS * probe_count)) / (weight_total * weight_total)
    return (own_images.astype(jnp.bfloat16), traces, energy / weight_total)


def solution(mesh):
    in_specs = (P("samp", "snp"), P("samp"), P("samp", None), P("samp"), P())
    out_specs = (P(("samp", "snp"), None), P(), P())
    return jax.shard_map(
        on_device, mesh=mesh, in_specs=in_specs, out_specs=out_specs, check_vma=False
    )
```

profile of v0, /device:TPU:0, one launch (start us, length us, event | category | flops | bytes accessed | tf_op | source)
XLA Modules:
  0.0 172.9 jit_solution(4429881836668498962)
XLA Ops:
  7.2 0.0 copy-start
  7.2 0.0 all-reduce.3.cloned.1.call-start
  7.2 1.1 copy.42
  8.3 1.3 convert_reduce_fusion.2
  9.6 0.1 shift_right_arithmetic.43
  9.7 0.7 fusion.1
  10.4 0.0 copy-done
  10.4 0.7 convolution_bitcast_fusion
  11.2 0.0 copy-start.1
  11.2 0.0 copy-start.2
  11.2 1.1 copy.55
  12.3 0.0 all-reduce.3.cloned.1.call-update
  12.3 0.0 reduce-scatter.4.cloned.1.call-start
  12.4 0.0 copy-done.1
  12.4 0.1 convert_reduce_fusion
  12.5 0.0 copy-done.2
  12.5 0.1 convert_reduce_fusion.1
  12.7 0.6 fusion.7
  13.3 0.7 fusion.18
  14.0 1.4 pad_maximum_fusion.1
  15.4 40.4 %all-reduce = (f32[66]{0:T(128)S(1)}, f32[3,4096]{1,0:T(4,128)S(1)}) all-reduce(f32[66]{0:T(128)S(1)} %pad_maximum_fusion.1, f32[3,4096]{1,0:T(4,128)S(1)} %pad_maximum_fusion), channel_id=1, replica_groups=mesh['samp'=8,'snp'=4] {'samp'}, use_global_device_ids=true, to_apply=%region_4.0 | all-reduce | flops 12354 | bytes 98832 | tf_op jit(solution)/shard_map/psum | solution.py:73
  55.9 0.1 slice.30
  55.9 0.6 fusion.28
  56.5 0.1 shift_right_arithmetic.49
  56.6 0.1 constant_dynamic-slice_fusion
  56.7 0.1 copy.35
  56.8 2.5 %shift_right_arithmetic.41 = s32[256,2,16,128]{0,3,2,1:T(8,128)} broadcast(s32[256,2,128]{0,2,1:T(8,128)S(1)} %bitcast.41), dimensions={0,1,3} | broadcast | bytes 4456448 | tf_op jit(solution)/shard_map/shift_right_arithmetic | solution.py:17
  59.2 5.6 %copy.36 = s32[256,32,128]{2,0,1:T(8,128)} copy(s32[256,32,128]{0,2,1:T(8,128)} %bitcast.38) | data formatting | bytes 8388608 | tf_op jit(solution)/shard_map/shift_right_arithmetic | solution.py:17
  64.8 0.1 multiply_reduce_fusion.2
  64.9 0.7 fusion.26
  65.6 0.7 multiply_multiply_fusion
  66.3 28.1 %all-reduce.3.cloned.1.call-done = f32[32,128,64]{1,2,0:T(8,128)} async-done(((f32[32,128,64]{1,2,0:T(8,128)}), f32[32,128,64]{1,2,0:T(8,128)}) %all-reduce.3.cloned.1.call-update) | async-done | bytes 1048592 | tf_op jit(solution)/shard_map/psum | solution.py:73
  94.4 1.7 multiply_reduce_fusion
  96.0 3.1 %subtract_bitcast_fusion = f32[256,32,64]{0,2,1:T(8,128)S(1)} fusion(bf16[32,128,64]{1,2,0:T(8,128)(2,1)S(1)} %get-tuple-element.18, s32[256,32,128]{2,0,1:T(8,128)} %copy.36, s32[32]{0:T(128)S(1)} %shift_right_arithmetic.49, f32[32,64]{1,0:T(8,128)S(1)} %get-tuple-element.17), kind=kOutput, calls=%fused_computation.7 | convolution fusion | flops 137887744 | bytes 6824064 | tf_op jit(solution)/shard_map/rtj,tjb->rtb/dot_general | solution.py:88
  99.1 2.0 %fusion.12 = f32[256,8,64]{0,1,2:T(8,128)S(1)} fusion(f32[256,32,64]{0,2,1:T(8,128)S(1)} %subtract_bitcast_fusion, f32[256]{0:T(256)S(1)} %get-tuple-element.29, pred[128,8]{0,1:T(8,128)(4,1)S(1)} %get-tuple-element.32, s32[]{:T(128)S(6)} %select_n.3), kind=kOutput, calls=%fused_computation.14 | convolution fusion | flops 50462720 | bytes 2623492 | tf_op jit(solution)/shard_map/rtb,tk->rkb/dot_general | solution.py:91
  101.1 0.2 copy.38
  101.3 1.0 copy.43
  102.3 0.0 reduce-scatter.4.cloned.1.call-update
  102.3 0.2 multiply_reduce_fusion.1
  102.5 6.5 %psum.39 = f32[8]{0:T(128)S(1)} all-reduce(f32[8]{0:T(128)S(1)} %multiply_reduce_fusion.1), channel_id=1, replica_groups=mesh['samp'=8,'snp'=4] {'snp'}, use_global_device_ids=true, to_apply=%region_12.0 | all-reduce | flops 8 | bytes 64 | tf_op jit(solution)/shard_map/psum | solution.py:79
  110.3 1.2 broadcast_divide_fusion
  111.5 12.2 %reduce-scatter.4.cloned.1.call-done = f32[64,512]{1,0:T(8,128)} async-done(((f32[256,512]{1,0:T(8,128)}), f32[64,512]{1,0:T(8,128)}) %reduce-scatter.4.cloned.1.call-update) | async-done | bytes 131088
  123.7 1.0 copy.44
  124.7 0.7 convolution_bitcast_fusion.1
  125.5 39.3 %psum.38 = f32[8,8]{1,0:T(8,128)S(1)} all-reduce(f32[8,8]{1,0:T(8,128)S(1)} %convolution_bitcast_fusion.1), channel_id=1, replica_groups=mesh['samp'=8,'snp'=4] {'samp','snp'}, use_global_device_ids=true, to_apply=%region_10.0 | all-reduce | flops 64 | bytes 512 | tf_op jit(solution)/shard_map/psum | solution.py:99
  164.8 0.7 copy.41
  165.5 0.6 multiply_divide_fusion
  (10 shorter events, 0.1 us)
Async XLA Ops:
  7.2 3.3 %copy-start = (bf16[256,64]{0,1:T(8,128)(2,1)S(1)}, bf16[256,64]{0,1:T(8,128)(2,1)}, u32[]{:S(2)}) copy-start(bf16[256,64]{0,1:T(8,128)(2,1)} %param.7) | copy-start | bytes 98308
  7.2 87.2 %all-reduce.3.cloned.1.call-start = ((), (), s32[]{:S(2)}) async-start(), calls=%async_computation.1 | async-start | bytes 2097152 | tf_op jit(solution)/shard_map/psum | solution.py:73
  11.2 1.2 copy-start.1
  11.2 1.3 copy-start.2
  12.3 111.4 %reduce-scatter.4.cloned.1.call-start = ((), (), s32[]{:S(2)}) async-start(), calls=%async_computation.2 | async-start | bytes 655360
Sparse Core Ops, SparseCore 0:
  12.4 81.8 all-reduce.2
  102.4 21.2 reduce-scatter.3
where the time goes:
time: 173 us
  blocking collectives  86.2 us (50%)
  waiting for transfers between devices  40.3 us (23%)
  between operations  15.5 us (9%)
  local copies, waits for them, and re-layouts  14.2 us (8%)
  other arithmetic  8.78 us (5%)
  matrix products  7.85 us (5%)
    psum x1, blocking collectives, on_device(): lax.psum((cross_panel.reshape(-1, 128), moments, totals), 'samp')  40.4 us
    psum x1, blocking collectives, on_device(): trace_sum = lax.psum(local_trace, ('samp', 'snp'))  39.3 us
    psum x1, waiting for transfers between devices, on_device(): lax.psum((cross_panel.reshape(-1, 128), moments, totals), 'samp')  28.1 us
    unnamed x3, waiting for transfers between devices  12.2 us
    shift_right_arithmetic x6, local copies, waits for them, and re-layouts, unpack_rows(): fields = jnp.right_shift(grouped, shifts) & 3  9.3 us
    psum x1, blocking collectives, on_device(): energy = lax.psum(energy, 'snp')  6.51 us
  transfers between devices with their start and end apart: 2, of which 2 were waited for; matrix products, arithmetic and copies ran while one was open for 9% of the time, Pallas kernels for 0%

commit v1 on v0

--- a/solution.py
+++ b/solution.py
@@ -1,6 +1,9 @@
+import functools
 import jax
 import jax.numpy as jnp
 from jax import lax
+from jax.experimental import pallas as pl
+from jax.experimental.pallas import tpu as pltpu
 from jax.sharding import PartitionSpec as P
 
 SNPS = 16384
@@ -102,9 +105,369 @@
     return (own_images.astype(jnp.bfloat16), traces, energy / weight_total)
 
 
+MESH = pl.DeviceIdType.MESH
+HIGHEST = lax.Precision.HIGHEST
+
+
+def whole_kernel(
+    sizes,
+    tile_smem,
+    words_ref,
+    counts_ref,
+    probes_ref,
+    pheno_ref,
+    tile_ref,
+    images_ref,
+    traces_ref,
+    yky_ref,
+    dosage,
+    panel_out,
+    moment_out,
+    panel_in,
+    moment_in,
+    coef,
+    spread_coef,
+    total,
+    piece_out,
+    piece_in,
+    sum_samp,
+    sum_snp,
+    sum_mid,
+    send_panel,
+    recv_panel,
+    send_moment,
+    recv_moment,
+    send_coef,
+    recv_coef,
+    send_piece,
+    recv_piece,
+    send_samp,
+    recv_samp,
+    send_snp,
+    recv_snp,
+):
+    n_samp, n_snp, tiles_local, probe_count = sizes
+    me, mine = lax.axis_index("samp"), lax.axis_index("snp")
+    chunk_tiles = tiles_local // n_samp
+    width = chunk_tiles * 128
+    height = words_ref.shape[0]
+    rows = height // n_snp
+    panel_rows = probe_count
+    f32, bf16 = jnp.float32, jnp.bfloat16
+
+    def samp_peer(offset):
+        return lax.rem(me + offset, n_samp)
+
+    def snp_peer(offset):
+        return lax.rem(mine + offset, n_snp)
+
+    barrier = pltpu.get_barrier_semaphore()
+    for o in range(1, n_samp):
+        pl.semaphore_signal(barrier, inc=1, device_id={"samp": samp_peer(o)}, device_id_type=MESH)
+    for o in range(1, n_snp):
+        pl.semaphore_signal(barrier, inc=1, device_id={"snp": snp_peer(o)}, device_id_type=MESH)
+
+    def remote(src, dst, send, recv, axis, peer):
+        return pltpu.make_async_remote_copy(
+            src_ref=src, dst_ref=dst, send_sem=send, recv_sem=recv,
+            device_id={axis: peer}, device_id_type=MESH,
+        )
+
+    weights = counts_ref[...].astype(f32)
+    root = jnp.sqrt(weights)
+    probe_t = probes_ref[...].astype(f32).T
+    probe_rows = (probe_t * root).astype(bf16)
+    pheno_rows = (pheno_ref[...] * root).astype(bf16)
+    low = lax.broadcasted_iota(jnp.int32, (16, height), 0)
+    extra = jnp.where(
+        low == 0, weights, jnp.where(low == 1, pheno_rows.astype(f32), 0.0)
+    ).astype(bf16)
+    left = jnp.concatenate([probe_rows, extra], axis=0)
+    count_left = jnp.where(low == 0, weights, 0.0).astype(bf16)
+
+    own_sums = jnp.sum(left.astype(f32), axis=1, keepdims=True)
+    own_column = own_sums[:panel_rows]
+    own_weight = own_sums[panel_rows:panel_rows + 1]
+    padded = jnp.concatenate(
+        [
+            jnp.broadcast_to(own_sums, (panel_rows + 16, 128)),
+            jnp.zeros((128 - panel_rows - 16, 128), f32),
+        ],
+        axis=0,
+    )
+    own_row = padded.T[0:1]
+    own_row_wide = jnp.concatenate([own_row] * chunk_tiles, axis=1)
+    own_scale = 1.0 / jnp.maximum(own_weight, 1.0)
+
+    own_panel = None
+    own_moment = None
+    order = list(range(1, n_samp)) + [0]
+    for step, o in enumerate(order):
+        owner = samp_peer(o)
+        pieces = []
+        for tt in range(chunk_tiles):
+            tile = owner * chunk_tiles + tt
+            group = lax.div(tile, 16)
+            shift = 2 * lax.rem(tile, 16)
+            words = words_ref[:, pl.ds(pl.multiple_of(group * 128, 128), 128)]
+            pieces.append((lax.shift_right_logical(words, jnp.broadcast_to(shift, words.shape)) & 3).astype(f32).astype(bf16))
+        x = jnp.concatenate(pieces, axis=1)
+        dosage[o, :height, :] = x
+        linear = jnp.dot(left, x, preferred_element_type=f32)
+        squares = jnp.dot(count_left, x * x, preferred_element_type=f32)
+        first = linear[panel_rows:panel_rows + 1]
+        panel = linear[:panel_rows] - own_column * (first * own_scale)
+        moment = jnp.concatenate(
+            [
+                first,
+                squares[0:1],
+                linear[panel_rows + 1:panel_rows + 2],
+                own_row_wide,
+                jnp.zeros((4, width), f32),
+            ],
+            axis=0,
+        )
+        if o == 0:
+            own_panel, own_moment = panel, moment
+        else:
+            panel_out[o] = panel.astype(bf16)
+            moment_out[o] = moment
+            if step == 0:
+                pl.semaphore_wait(barrier, n_samp + n_snp - 2)
+            remote(panel_out.at[o], panel_in.at[o], send_panel.at[o], recv_panel.at[o], "samp", owner).start()
+            remote(moment_out.at[o], moment_in.at[o], send_moment.at[o], recv_moment.at[o], "samp", owner).start()
+
+    root_wide = jnp.broadcast_to(root, (128, height)).T
+
+    moments = [own_moment]
+    panel_sum = own_panel
+    for o in range(1, n_samp):
+        remote(moment_out.at[o], moment_in.at[o], send_moment.at[o], recv_moment.at[o], "samp", samp_peer(o)).wait_recv()
+        remote(panel_out.at[o], panel_in.at[o], send_panel.at[o], recv_panel.at[o], "samp", samp_peer(o)).wait_recv()
+        moments.append(moment_in[o])
+        panel_sum = panel_sum + panel_in[o].astype(f32)
+    moment_sum = moments[0]
+    for item in moments[1:]:
+        moment_sum = moment_sum + item
+    row_stack = jnp.concatenate(
+        [item[3:4, :128] for item in moments] + [jnp.zeros((128 - n_samp, 128), f32)], axis=0
+    )
+    columns = row_stack.T
+    totals = jnp.sum(columns, axis=1, keepdims=True)
+    weight_total = totals[panel_rows:panel_rows + 1]
+    pheno_total = totals[panel_rows + 1:panel_rows + 2]
+    average = moment_sum[0:1] / weight_total
+    second = moment_sum[1:2] / weight_total
+    spread = 1.0 / jnp.sqrt(second - average * average + EPSILON)
+    shifts = []
+    for index, item in enumerate(moments):
+        own = columns[panel_rows:panel_rows + 1, index:index + 1]
+        shifts.append(item[0:1] * (1.0 / jnp.maximum(own, 1.0)) - average)
+    shifts.append(jnp.zeros((128 - n_samp, width), f32))
+    correction = jnp.dot(
+        columns[:panel_rows], jnp.concatenate(shifts, axis=0),
+        precision=HIGHEST, preferred_element_type=f32,
+    )
+    unit_panel = spread * (panel_sum + correction)
+    pheno_unit = spread * (moment_sum[2:3] - average * pheno_total)
+
+    tile_all = tile_ref[...]
+    inverse_parts = []
+    lanes = lax.broadcasted_iota(jnp.int32, (1, 128), 1)
+    tile_first = mine * tiles_local
+    own_tiles = [tile_smem[tile_first + me * chunk_tiles + tt] for tt in range(chunk_tiles)]
+    for tt in range(chunk_tiles):
+        size = 128.0 * jnp.sum((tile_all == own_tiles[tt]).astype(f32), axis=1, keepdims=True)
+        inverse_parts.append(jnp.broadcast_to(1.0 / size, (1, 128)))
+    inverse = jnp.concatenate(inverse_parts, axis=1)
+    coefficients = (spread * unit_panel * inverse).astype(bf16)
+    high = average.astype(bf16).astype(f32)
+    rest = average - high
+    middle = rest.astype(bf16).astype(f32)
+    last = rest - middle
+    low_wide = lax.broadcasted_iota(jnp.int32, (16, width), 0)
+    average_rows = jnp.where(
+        low_wide == 0, high, jnp.where(low_wide == 1, middle, jnp.where(low_wide == 2, last, 0.0))
+    ).astype(bf16)
+    coef[0, :panel_rows, :] = coefficients
+    coef[0, panel_rows:, :] = average_rows
+    for o in range(1, n_samp):
+        remote(coef.at[0], coef.at[n_samp - o], send_coef.at[o], recv_coef.at[n_samp - o], "samp", samp_peer(o)).start()
+
+    energy_snps = pheno_unit * pheno_unit * inverse
+    energy = jnp.zeros((1, 128), f32)
+    for tt in range(chunk_tiles):
+        part = jnp.sum(energy_snps[:, tt * 128:(tt + 1) * 128], axis=1, keepdims=True)
+        energy = energy + jnp.where(lanes == own_tiles[tt], part, 0.0)
+
+    wide_lane = lax.broadcasted_iota(jnp.int32, (1, width), 1)
+    wait_order = [0]
+    for o in range(1, n_samp // 2 + 1):
+        wait_order.append(o)
+        if n_samp - o != o:
+            wait_order.append(n_samp - o)
+    for step, s in enumerate(wait_order):
+        owner = samp_peer(s)
+        if s != 0:
+            remote(coef.at[0], coef.at[s], send_coef.at[s], recv_coef.at[s], "samp", owner).wait_recv()
+        comp = jnp.zeros((1, width), jnp.int32)
+        for tt in range(chunk_tiles):
+            number = tile_smem[tile_first + owner * chunk_tiles + tt]
+            comp = jnp.where(lax.div(wide_lane, 128) == tt, number, comp)
+        part = coef[s, :panel_rows, :]
+        for k in range(COMPS):
+            mask = (comp == k).astype(f32).astype(bf16)
+            spread_coef[step % 2, k * panel_rows:(k + 1) * panel_rows, :] = part * mask
+        dosage[s, height:, :] = coef[s, panel_rows:, :]
+        product = lax.dot_general(
+            dosage[s], spread_coef[step % 2], (((1,), (1,)), ((), ())), preferred_element_type=f32
+        )
+        if step == 0:
+            total[...] = product
+        else:
+            total[...] += product
+
+    centre = total[height:height + 1, :] + (total[height + 1:height + 2, :] + total[height + 2:height + 3, :])
+    total[:height, :] = (total[:height, :] - centre) * jnp.concatenate(
+        [root_wide] * (COMPS * probe_count // 128), axis=1
+    )
+    for o in range(1, n_snp):
+        peer = snp_peer(o)
+        piece_out[o] = total[pl.ds(pl.multiple_of(peer * rows, rows), rows), :].astype(bf16)
+        remote(piece_out.at[o], piece_in.at[o], send_piece.at[o], recv_piece.at[o], "snp", peer).start()
+    image = total[pl.ds(pl.multiple_of(mine * rows, rows), rows), :]
+    for o in range(1, n_snp):
+        remote(piece_out.at[o], piece_in.at[o], send_piece.at[o], recv_piece.at[o], "snp", snp_peer(o)).wait_recv()
+        image = image + piece_in[o].astype(f32)
+    images_ref[...] = image.astype(bf16)
+
+    span = COMPS * probe_count
+    turned = pltpu.roll(image, span - probe_count, 1)
+    sums = []
+    for d in range(COMPS):
+        base = image if d % 2 == 0 else turned
+        cut = (d // 2) * 2 * probe_count
+        other = base if cut == 0 else jnp.concatenate([base[:, cut:], base[:, :cut]], axis=1)
+        sums.append(jnp.sum(image * other, axis=0, keepdims=True))
+    stacked = jnp.concatenate(sums, axis=0)
+    picker = (
+        lax.div(lax.broadcasted_iota(jnp.int32, (span, 128), 0), probe_count)
+        == lax.broadcasted_iota(jnp.int32, (span, 128), 1)
+    ).astype(f32)
+    pairs = jnp.dot(stacked, picker, precision=HIGHEST, preferred_element_type=f32)
+
+    sum_samp[me, 0:COMPS, :] = pairs
+    sum_samp[me, COMPS:, :] = jnp.broadcast_to(energy, (8, 128))
+    for o in range(1, n_samp):
+        remote(sum_samp.at[me], sum_samp.at[me], send_samp.at[o], recv_samp.at[o], "samp", samp_peer(o)).start()
+    for o in range(1, n_samp):
+        source = lax.rem(me + n_samp - o, n_samp)
+        remote(sum_samp.at[source], sum_samp.at[source], send_samp.at[o], recv_samp.at[o], "samp", samp_peer(o)).wait_recv()
+    group_sum = sum_samp[0]
+    for i in range(1, n_samp):
+        group_sum = group_sum + sum_samp[i]
+    sum_mid[...] = group_sum
+    for o in range(1, n_snp):
+        remote(sum_mid, sum_snp.at[mine], send_snp.at[o], recv_snp.at[o], "snp", snp_peer(o)).start()
+    sum_snp[mine] = group_sum
+    for o in range(1, n_snp):
+        source = lax.rem(mine + n_snp - o, n_snp)
+        remote(sum_mid, sum_snp.at[source], send_snp.at[o], recv_snp.at[o], "snp", snp_peer(o)).wait_recv()
+    everything = sum_snp[0]
+    for i in range(1, n_snp):
+        everything = everything + sum_snp[i]
+    row_id = lax.broadcasted_iota(jnp.int32, (COMPS, 128), 0)
+    lane_id = lax.broadcasted_iota(jnp.int32, (COMPS, 128), 1)
+    turn = (row_id - lane_id) & (COMPS - 1)
+    trace = jnp.zeros((COMPS, 128), f32)
+    for d in range(COMPS):
+        trace = jnp.where(turn == d, everything[d:d + 1], trace)
+    trace = trace * (SNPS / (COMPS * probe_count)) / (weight_total * weight_total)
+    traces_ref[...] = trace[:, :COMPS]
+    yky_ref[...] = (everything[COMPS:COMPS + 1] / weight_total)[:, :COMPS]
+
+    for o in range(1, n_samp):
+        remote(panel_out.at[o], panel_in.at[o], send_panel.at[o], recv_panel.at[o], "samp", samp_peer(o)).wait_send()
+        remote(moment_out.at[o], moment_in.at[o], send_moment.at[o], recv_moment.at[o], "samp", samp_peer(o)).wait_send()
+        remote(coef.at[0], coef.at[n_samp - o], send_coef.at[o], recv_coef.at[n_samp - o], "samp", samp_peer(o)).wait_send()
+        remote(sum_samp.at[me], sum_samp.at[me], send_samp.at[o], recv_samp.at[o], "samp", samp_peer(o)).wait_send()
+    for o in range(1, n_snp):
+        remote(piece_out.at[o], piece_in.at[o], send_piece.at[o], recv_piece.at[o], "snp", snp_peer(o)).wait_send()
+        remote(sum_mid, sum_snp.at[mine], send_snp.at[o], recv_snp.at[o], "snp", snp_peer(o)).wait_send()
+
+
+def on_device_fused(geno_words, counts, probes, phenotype, tile_comp):
+    n_samp, n_snp = lax.axis_size("samp"), lax.axis_size("snp")
+    height = geno_words.shape[0]
+    tiles_local = geno_words.shape[1] * 16 // 128
+    probe_count = probes.shape[1]
+    width = tiles_local // n_samp * 128
+    span = COMPS * probe_count
+    rows = height // n_snp
+    f32, bf16 = jnp.float32, jnp.bfloat16
+    vmem = pl.BlockSpec(memory_space=pltpu.VMEM)
+    smem = pl.BlockSpec(memory_space=pltpu.SMEM)
+    dma = pltpu.SemaphoreType.DMA
+    images, traces, yky = pl.pallas_call(
+        functools.partial(whole_kernel, (n_samp, n_snp, tiles_local, probe_count)),
+        out_shape=(
+            jax.ShapeDtypeStruct((rows, span), bf16),
+            jax.ShapeDtypeStruct((COMPS, COMPS), f32),
+            jax.ShapeDtypeStruct((1, COMPS), f32),
+        ),
+        in_specs=[smem] + [vmem] * 5,
+        out_specs=(vmem, vmem, vmem),
+        scratch_shapes=[
+            pltpu.VMEM((n_samp, height + 16, width), bf16),
+            pltpu.VMEM((n_samp, probe_count, width), bf16),
+            pltpu.VMEM((n_samp, 8, width), f32),
+            pltpu.VMEM((n_samp, probe_count, width), bf16),
+            pltpu.VMEM((n_samp, 8, width), f32),
+            pltpu.VMEM((n_samp, probe_count + 16, width), bf16),
+            pltpu.VMEM((2, span, width), bf16),
+            pltpu.VMEM((height + 16, span), f32),
+            pltpu.VMEM((n_snp, rows, span), bf16),
+            pltpu.VMEM((n_snp, rows, span), bf16),
+            pltpu.VMEM((n_samp, COMPS + 8, 128), f32),
+            pltpu.VMEM((n_snp, COMPS + 8, 128), f32),
+            pltpu.VMEM((COMPS + 8, 128), f32),
+            dma((n_samp,)),
+            dma((n_samp,)),
+            dma((n_samp,)),
+            dma((n_samp,)),
+            dma((n_samp,)),
+            dma((n_samp,)),
+            dma((n_snp,)),
+            dma((n_snp,)),
+            dma((n_samp,)),
+            dma((n_samp,)),
+            dma((n_snp,)),
+            dma((n_snp,)),
+        ],
+        compiler_params=pltpu.CompilerParams(collective_id=0, has_side_effects=True),
+    )(
+        tile_comp,
+        geno_words,
+        counts.reshape(1, -1),
+        probes,
+        phenotype.reshape(1, -1),
+        tile_comp.reshape(1, -1),
+    )
+    return (images, traces, yky.reshape(-1))
+
+
+def dispatch(geno_words, counts, probes, phenotype, tile_comp):
+    n_samp, n_snp = lax.axis_size("samp"), lax.axis_size("snp")
+    tiles_local = geno_words.shape[1] * 16 // 128
+    whole_tiles = tiles_local % n_samp == 0 and tile_comp.shape[0] == 128
+    whole_rows = geno_words.shape[0] % (16 * n_snp) == 0 and probes.shape[1] == 64
+    body = on_device_fused if whole_tiles and whole_rows else on_device
+    return body(geno_words, counts, probes, phenotype, tile_comp)
+
+
 def solution(mesh):
     in_specs = (P("samp", "snp"), P("samp"), P("samp", None), P("samp"), P())
     out_specs = (P(("samp", "snp"), None), P(), P())
     return jax.shard_map(
-        on_device, mesh=mesh, in_specs=in_specs, out_specs=out_specs, check_vma=False
-    )
+        dispatch, mesh=mesh, in_specs=in_specs, out_specs=out_specs, check_vma=False
+    )

time: 173 us -> 58.9 us (0.34)
  blocking collectives: 86.2 us -> 0 us
  Pallas kernels: 0 us -> 53.9 us
  waiting for transfers between devices: 40.3 us -> 0 us
  between operations: 15.5 us -> 0.65 us
  local copies, waits for them, and re-layouts: 14.2 us -> 4.08 us
  other arithmetic: 8.78 us -> 0 us
  matrix products: 7.85 us -> 0 us
    psum x3 -> x0, blocking collectives: 86.2 us -> none  [the longest x1 40.4 us: on_device(): lax.psum((cross_panel.reshape(-1, 128), moments, totals), 'samp')]
    pallas_call x0 -> x1, Pallas kernels: none -> 53.9 us  [on_device_fused(): pl.pallas_call(functools.partial(whole_kernel, (n_samp, n_snp, tiles_loca...]
    psum x1 -> x0, waiting for transfers between devices: 28.1 us -> none  [on_device(): lax.psum((cross_panel.reshape(-1, 128), moments, totals), 'samp')]
    unnamed x3 -> x0, waiting for transfers between devices: 12.2 us -> none
    shift_right_arithmetic x6 -> x0, local copies, waits for them, and re-layouts: 9.3 us -> none  [unpack_rows(): fields = jnp.right_shift(grouped, shifts) & 3]
    dot_general x6 -> x0, matrix products: 7.85 us -> none  [the longest x1 3.11 us: on_device(): jnp.einsum('rtj,tjb->rtb', dosage, coef_tiles, preferred_element_type=jnp...]
    reduce_sum x6 -> x0, other arithmetic: 3.51 us -> none  [the longest x1 1.66 us: on_device(): jnp.sum(average.reshape(tile_local, 128, 1) * coef_tiles.astype(jnp.float...]
    div x3 -> x0, other arithmetic: 1.77 us -> none  [the longest x1 1.16 us: on_device(): return (own_images.astype(jnp.bfloat16), traces, energy / weight_total)]
  transfers between devices with their start and end apart: 2 -> 0, of which waited for: 2 -> 0; matrix products, arithmetic and copies ran while one was open for 9% -> 0% of each run, Pallas kernels for 0% -> 0%
where the time goes in v1:
time: 58.9 us; the launch traced here: 58.6 us
  Pallas kernels  53.9 us (92%)
  local copies, waits for them, and re-layouts  4.08 us (7%)
  between operations  0.65 us (1%)
    pallas_call x1, Pallas kernels, on_device_fused(): pl.pallas_call(functools.partial(whole_kernel, (n_samp, n_snp, tiles_loca...  53.9 us
    unnamed x8, local copies, waits for them, and re-layouts  4.08 us

profile of v1, /device:TPU:0, one launch (start us, length us, event | category | flops | bytes accessed | tf_op | source)
XLA Modules:
  0.0 58.6 jit_solution(16066551619139064030)
XLA Ops:
  0.6 1.5 %copy.8.probes_ref = bf16[256,64]{1,0:T(8,128)(2,1)} copy(bf16[256,64]{0,1:T(8,128)(2,1)} %param.7) | data formatting | bytes 65536 | tf_op args[2]
  2.1 53.9 %shard_map.76 = (bf16[64,512]{1,0:T(8,128)(2,1)}, f32[8,8]{1,0:T(8,128)}, f32[1,8]{1,0:T(1,128)}) custom-call(s32[128]{0:T(128)} %tile_smem.1, s32[256,256]{1,0:T(8,128)} %words_ref.1, s32[1,256]{1,0:T(1,128)} %bitcast.5, bf16[256,64]{1,0:T(8,128)(2,1)} %copy.8.probes_ref, f32[1,256]{1,0:T(1,128)} %bitcast.6, s32[1,128]{1,0:T(1,128)} %bitcast.4), custom_call_target="tpu_custom_call" | custom-call | tf_op jit(solution)/shard_map/pallas_call | solution.py:411
  56.0 0.0 copy-start
  56.0 1.5 %copy.12 = bf16[64,512]{1,0:T(8,128)(2,1)} copy(bf16[64,512]{1,0:T(8,128)(2,1)} %get-tuple-element.12) | data formatting | bytes 131072
  57.5 0.0 copy-done
  57.5 0.0 copy-start.1
  57.5 0.6 %copy.13 = f32[8,8]{1,0:T(8,128)} copy(f32[8,8]{1,0:T(8,128)S(1)} %copy-done) | data formatting | bytes 512
  58.1 0.0 copy-done.1
  58.1 0.5 copy.14
Async XLA Ops:
  56.0 1.5 %copy-start = (f32[8,8]{1,0:T(8,128)S(1)}, f32[8,8]{1,0:T(8,128)}, u32[]{:S(2)}) copy-start(f32[8,8]{1,0:T(8,128)} %get-tuple-element.13) | copy-start | bytes 772
  57.5 0.6 %copy-start.1 = (f32[1,8]{1,0:T(1,128)S(1)}, f32[1,8]{1,0:T(1,128)}, u32[]{:S(2)}) copy-start(f32[1,8]{1,0:T(1,128)} %get-tuple-element.8) | copy-start | bytes 100

commit v2 on v1

--- a/solution.py
+++ b/solution.py
@@ -107,6 +107,8 @@
 
 MESH = pl.DeviceIdType.MESH
 HIGHEST = lax.Precision.HIGHEST
+HALVES = 2
+PAIR = 2
 
 
 def whole_kernel(
@@ -121,11 +123,17 @@
     traces_ref,
     yky_ref,
     dosage,
-    panel_out,
-    moment_out,
-    panel_in,
-    moment_in,
+    keep,
+    pair_out,
+    pair_note_out,
+    pair_in,
+    pair_note_in,
+    line_out,
+    line_note_out,
+    line_in,
+    line_note_in,
     coef,
+    means,
     spread_coef,
     total,
     piece_out,
@@ -133,12 +141,18 @@
     sum_samp,
     sum_snp,
     sum_mid,
-    send_panel,
-    recv_panel,
-    send_moment,
-    recv_moment,
+    send_pair,
+    recv_pair,
+    send_pair_note,
+    recv_pair_note,
+    send_line,
+    recv_line,
+    send_line_note,
+    recv_line_note,
     send_coef,
     recv_coef,
+    send_means,
+    recv_means,
     send_piece,
     recv_piece,
     send_samp,
@@ -146,10 +160,15 @@
     send_snp,
     recv_snp,
 ):
-    n_samp, n_snp, tiles_local, probe_count = sizes
+    n_samp, n_snp, tiles_local, probe_count, halves = sizes
     me, mine = lax.axis_index("samp"), lax.axis_index("snp")
+    n_line = n_samp // PAIR
+    line, side = lax.div(me, PAIR), lax.rem(me, PAIR)
+    partner = line * PAIR + (1 - side)
     chunk_tiles = tiles_local // n_samp
-    width = chunk_tiles * 128
+    block_tiles = chunk_tiles // halves
+    width = block_tiles * 128
+    note_rows = pair_note_in.shape[2]
     height = words_ref.shape[0]
     rows = height // n_snp
     panel_rows = probe_count
@@ -160,6 +179,15 @@
 
     def snp_peer(offset):
         return lax.rem(mine + offset, n_snp)
+
+    def line_peer(offset):
+        return lax.rem(line + offset, n_line) * PAIR + side
+
+    def owner_of(offset, other):
+        return lax.rem(line + offset, n_line) * PAIR + (1 - side if other else side)
+
+    far_first = sorted(range(1, n_line), key=lambda o: -min(o, n_line - o))
+    near_first = sorted(range(1, n_line), key=lambda o: min(o, n_line - o))
 
     barrier = pltpu.get_barrier_semaphore()
     for o in range(1, n_samp):
@@ -173,10 +201,49 @@
             device_id={axis: peer}, device_id_type=MESH,
         )
 
+    def pair_copies(h, o):
+        return (
+            remote(pair_out.at[h, o], pair_in.at[h, o], send_pair.at[h, o], recv_pair.at[h, o], "samp", partner),
+            remote(pair_note_out.at[h, o], pair_note_in.at[h, o], send_pair_note.at[h, o], recv_pair_note.at[h, o], "samp", partner),
+        )
+
+    def line_copies(h, o):
+        return (
+            remote(line_out.at[h, o], line_in.at[h, o], send_line.at[h, o], recv_line.at[h, o], "samp", line_peer(o)),
+            remote(line_note_out.at[h, o], line_note_in.at[h, o], send_line_note.at[h, o], recv_line_note.at[h, o], "samp", line_peer(o)),
+        )
+
+    def coef_copies(h, source, target, send, peer):
+        return (
+            remote(coef.at[h, source], coef.at[h, target], send_coef.at[h, send], recv_coef.at[h, target], "samp", peer),
+            remote(means.at[h, source], means.at[h, target], send_means.at[h, send], recv_means.at[h, target], "samp", peer),
+        )
+
+    def start(copies):
+        for item in copies:
+            item.start()
+
+    def received(copies):
+        for item in copies:
+            item.wait_recv()
+
+    def note_of(first, second, third, last):
+        parts = [v[:, t * 128:(t + 1) * 128] for v in (first, second, third) for t in range(block_tiles)]
+        parts.append(last)
+        spare = note_rows - len(parts)
+        if spare:
+            parts.append(jnp.zeros((spare, 128), f32))
+        return jnp.concatenate(parts, axis=0)
+
+    def wide_of(note, row):
+        return jnp.concatenate([note[row * block_tiles + t:row * block_tiles + t + 1] for t in range(block_tiles)], axis=1)
+
+    def last_of(note):
+        return note[3 * block_tiles:3 * block_tiles + 1]
+
     weights = counts_ref[...].astype(f32)
     root = jnp.sqrt(weights)
-    probe_t = probes_ref[...].astype(f32).T
-    probe_rows = (probe_t * root).astype(bf16)
+    probe_rows = (probes_ref[...].astype(f32) * root).astype(bf16)
     pheno_rows = (pheno_ref[...] * root).astype(bf16)
     low = lax.broadcasted_iota(jnp.int32, (16, height), 0)
     extra = jnp.where(
@@ -196,131 +263,169 @@
         axis=0,
     )
     own_row = padded.T[0:1]
-    own_row_wide = jnp.concatenate([own_row] * chunk_tiles, axis=1)
     own_scale = 1.0 / jnp.maximum(own_weight, 1.0)
 
-    own_panel = None
-    own_moment = None
-    order = list(range(1, n_samp)) + [0]
-    for step, o in enumerate(order):
-        owner = samp_peer(o)
+    def block(h, o, other):
+        owner = owner_of(o, other)
         pieces = []
-        for tt in range(chunk_tiles):
-            tile = owner * chunk_tiles + tt
+        for tt in range(block_tiles):
+            tile = owner * chunk_tiles + h * block_tiles + tt
             group = lax.div(tile, 16)
             shift = 2 * lax.rem(tile, 16)
             words = words_ref[:, pl.ds(pl.multiple_of(group * 128, 128), 128)]
-            pieces.append((lax.shift_right_logical(words, jnp.broadcast_to(shift, words.shape)) & 3).astype(f32).astype(bf16))
+            field = lax.shift_right_logical(words, jnp.broadcast_to(shift, words.shape)) & 3
+            pieces.append(field.astype(f32).astype(bf16))
         x = jnp.concatenate(pieces, axis=1)
-        dosage[o, :height, :] = x
+        dosage[h, o * PAIR + other, :height, :] = x
         linear = jnp.dot(left, x, preferred_element_type=f32)
         squares = jnp.dot(count_left, x * x, preferred_element_type=f32)
         first = linear[panel_rows:panel_rows + 1]
-        panel = linear[:panel_rows] - own_column * (first * own_scale)
-        moment = jnp.concatenate(
-            [
-                first,
-                squares[0:1],
-                linear[panel_rows + 1:panel_rows + 2],
-                own_row_wide,
-                jnp.zeros((4, width), f32),
-            ],
-            axis=0,
-        )
-        if o == 0:
-            own_panel, own_moment = panel, moment
-        else:
-            panel_out[o] = panel.astype(bf16)
-            moment_out[o] = moment
-            if step == 0:
+        middle = first * own_scale
+        panel = linear[:panel_rows] - own_column * middle
+        return panel, first, squares[0:1], linear[panel_rows + 1:panel_rows + 2], middle
+
+    waited = False
+    for h in range(halves):
+        for o in far_first + [0]:
+            panel, first, square, cross, middle = block(h, o, 1)
+            pair_out[h, o] = panel.astype(bf16)
+            pair_note_out[h, o] = note_of(first, square, cross, own_row)
+            if not waited:
                 pl.semaphore_wait(barrier, n_samp + n_snp - 2)
-            remote(panel_out.at[o], panel_in.at[o], send_panel.at[o], recv_panel.at[o], "samp", owner).start()
-            remote(moment_out.at[o], moment_in.at[o], send_moment.at[o], recv_moment.at[o], "samp", owner).start()
-
+                waited = True
+            start(pair_copies(h, o))
+    own_notes = {}
+    for h in range(halves):
+        for o in far_first + [0]:
+            panel, first, square, cross, middle = block(h, o, 0)
+            keep[h, o] = panel
+            own_notes[h, o] = (first, square, cross, middle)
     root_wide = jnp.broadcast_to(root, (128, height)).T
 
-    moments = [own_moment]
-    panel_sum = own_panel
-    for o in range(1, n_samp):
-        remote(moment_out.at[o], moment_in.at[o], send_moment.at[o], recv_moment.at[o], "samp", samp_peer(o)).wait_recv()
-        remote(panel_out.at[o], panel_in.at[o], send_panel.at[o], recv_panel.at[o], "samp", samp_peer(o)).wait_recv()
-        moments.append(moment_in[o])
-        panel_sum = panel_sum + panel_in[o].astype(f32)
-    moment_sum = moments[0]
-    for item in moments[1:]:
-        moment_sum = moment_sum + item
-    row_stack = jnp.concatenate(
-        [item[3:4, :128] for item in moments] + [jnp.zeros((128 - n_samp, 128), f32)], axis=0
-    )
-    columns = row_stack.T
-    totals = jnp.sum(columns, axis=1, keepdims=True)
-    weight_total = totals[panel_rows:panel_rows + 1]
-    pheno_total = totals[panel_rows + 1:panel_rows + 2]
-    average = moment_sum[0:1] / weight_total
-    second = moment_sum[1:2] / weight_total
-    spread = 1.0 / jnp.sqrt(second - average * average + EPSILON)
-    shifts = []
-    for index, item in enumerate(moments):
-        own = columns[panel_rows:panel_rows + 1, index:index + 1]
-        shifts.append(item[0:1] * (1.0 / jnp.maximum(own, 1.0)) - average)
-    shifts.append(jnp.zeros((128 - n_samp, width), f32))
-    correction = jnp.dot(
-        columns[:panel_rows], jnp.concatenate(shifts, axis=0),
-        precision=HIGHEST, preferred_element_type=f32,
-    )
-    unit_panel = spread * (panel_sum + correction)
-    pheno_unit = spread * (moment_sum[2:3] - average * pheno_total)
+    other_column = None
+    own_pair = {}
+    for h in range(halves):
+        for o in far_first + [0]:
+            received(pair_copies(h, o))
+            note = pair_note_in[h, o]
+            if other_column is None:
+                other_row = last_of(note)
+                turned = jnp.broadcast_to(other_row, (128, 128)).T[:, 0:1]
+                other_column = turned[:panel_rows]
+                other_weight = turned[panel_rows:panel_rows + 1]
+                other_scale = 1.0 / jnp.maximum(other_weight, 1.0)
+                pair_scale = 1.0 / jnp.maximum(own_weight + other_weight, 1.0)
+                pair_row = own_row + other_row
+            first, square, cross, middle = own_notes[h, o]
+            other_first = wide_of(note, 0)
+            pair_first = first + other_first
+            pair_middle = pair_first * pair_scale
+            panel = (
+                keep[h, o]
+                + pair_in[h, o].astype(f32)
+                + own_column * (middle - pair_middle)
+                + other_column * (other_first * other_scale - pair_middle)
+            )
+            pair_note = (pair_first, square + wide_of(note, 1), cross + wide_of(note, 2))
+            if o == 0:
+                own_pair[h] = (panel, pair_note)
+            else:
+                line_out[h, o] = panel.astype(bf16)
+                line_note_out[h, o] = note_of(*pair_note, pair_row)
+                start(line_copies(h, o))
 
     tile_all = tile_ref[...]
-    inverse_parts = []
     lanes = lax.broadcasted_iota(jnp.int32, (1, 128), 1)
     tile_first = mine * tiles_local
     own_tiles = [tile_smem[tile_first + me * chunk_tiles + tt] for tt in range(chunk_tiles)]
+    inverse_parts = []
     for tt in range(chunk_tiles):
         size = 128.0 * jnp.sum((tile_all == own_tiles[tt]).astype(f32), axis=1, keepdims=True)
         inverse_parts.append(jnp.broadcast_to(1.0 / size, (1, 128)))
-    inverse = jnp.concatenate(inverse_parts, axis=1)
-    coefficients = (spread * unit_panel * inverse).astype(bf16)
-    high = average.astype(bf16).astype(f32)
-    rest = average - high
-    middle = rest.astype(bf16).astype(f32)
-    last = rest - middle
+
+    columns = None
+    energy = jnp.zeros((1, 128), f32)
+    for h in range(halves):
+        panel_sum, own_note = own_pair[h]
+        notes = [own_note]
+        last_rows = [pair_row]
+        for o in far_first:
+            received(line_copies(h, o))
+            note = line_note_in[h, o]
+            panel_sum = panel_sum + line_in[h, o].astype(f32)
+            notes.append((wide_of(note, 0), wide_of(note, 1), wide_of(note, 2)))
+            last_rows.append(last_of(note))
+        if columns is None:
+            columns = jnp.concatenate(last_rows + [jnp.zeros((128 - n_line, 128), f32)], axis=0).T
+            totals = jnp.sum(columns, axis=1, keepdims=True)
+            weight_total = totals[panel_rows:panel_rows + 1]
+            pheno_total = totals[panel_rows + 1:panel_rows + 2]
+            part_scales = [
+                1.0 / jnp.maximum(columns[panel_rows:panel_rows + 1, i:i + 1], 1.0) for i in range(n_line)
+            ]
+        moment_sum = list(notes[0])
+        for item in notes[1:]:
+            moment_sum = [u + v for u, v in zip(moment_sum, item)]
+        average = moment_sum[0] / weight_total
+        second = moment_sum[1] / weight_total
+        spread = 1.0 / jnp.sqrt(second - average * average + EPSILON)
+        shifts = [item[0] * part_scales[i] - average for i, item in enumerate(notes)]
+        shifts.append(jnp.zeros((128 - n_line, width), f32))
+        correction = jnp.dot(
+            columns[:panel_rows], jnp.concatenate(shifts, axis=0),
+            precision=HIGHEST, preferred_element_type=f32,
+        )
+        unit_panel = spread * (panel_sum + correction)
+        pheno_unit = spread * (moment_sum[2] - average * pheno_total)
+        inverse = jnp.concatenate(inverse_parts[h * block_tiles:(h + 1) * block_tiles], axis=1)
+        coef[h, 0] = (spread * unit_panel * inverse).astype(bf16)
+        means[h, 0] = jnp.concatenate(
+            [average[:, t * 128:(t + 1) * 128] for t in range(block_tiles)]
+            + [jnp.zeros((8 - block_tiles, 128), f32)],
+            axis=0,
+        )
+        for o in far_first:
+            start(coef_copies(h, 0, (n_line - o) * PAIR, o, line_peer(o)))
+        start(coef_copies(h, 0, 1, 0, partner))
+        energy_snps = pheno_unit * pheno_unit * inverse
+        for t in range(block_tiles):
+            part = jnp.sum(energy_snps[:, t * 128:(t + 1) * 128], axis=1, keepdims=True)
+            energy = energy + jnp.where(lanes == own_tiles[h * block_tiles + t], part, 0.0)
+
+    wide_lane = lax.broadcasted_iota(jnp.int32, (1, width), 1)
     low_wide = lax.broadcasted_iota(jnp.int32, (16, width), 0)
-    average_rows = jnp.where(
-        low_wide == 0, high, jnp.where(low_wide == 1, middle, jnp.where(low_wide == 2, last, 0.0))
-    ).astype(bf16)
-    coef[0, :panel_rows, :] = coefficients
-    coef[0, panel_rows:, :] = average_rows
-    for o in range(1, n_samp):
-        remote(coef.at[0], coef.at[n_samp - o], send_coef.at[o], recv_coef.at[n_samp - o], "samp", samp_peer(o)).start()
-
-    energy_snps = pheno_unit * pheno_unit * inverse
-    energy = jnp.zeros((1, 128), f32)
-    for tt in range(chunk_tiles):
-        part = jnp.sum(energy_snps[:, tt * 128:(tt + 1) * 128], axis=1, keepdims=True)
-        energy = energy + jnp.where(lanes == own_tiles[tt], part, 0.0)
-
-    wide_lane = lax.broadcasted_iota(jnp.int32, (1, width), 1)
-    wait_order = [0]
-    for o in range(1, n_samp // 2 + 1):
-        wait_order.append(o)
-        if n_samp - o != o:
-            wait_order.append(n_samp - o)
-    for step, s in enumerate(wait_order):
-        owner = samp_peer(s)
-        if s != 0:
-            remote(coef.at[0], coef.at[s], send_coef.at[s], recv_coef.at[s], "samp", owner).wait_recv()
+    plan = []
+    for h in range(halves):
+        plan += [(h, 0, 0)] + [(h, o, 0) for o in near_first]
+        if h == 0:
+            plan += [(h, 0, 1)]
+    for h in range(halves):
+        plan += ([(h, 0, 1)] if h else []) + [(h, o, 1) for o in near_first]
+    for step, (h, o, other) in enumerate(plan):
+        slot = o * PAIR + other
+        if slot != 0:
+            received(coef_copies(h, 0, slot, 0, partner))
+            if other == 0:
+                start(coef_copies(h, slot, slot + 1, n_line + o, partner))
+        owner = owner_of(o, other)
         comp = jnp.zeros((1, width), jnp.int32)
-        for tt in range(chunk_tiles):
-            number = tile_smem[tile_first + owner * chunk_tiles + tt]
+        for tt in range(block_tiles):
+            number = tile_smem[tile_first + owner * chunk_tiles + h * block_tiles + tt]
             comp = jnp.where(lax.div(wide_lane, 128) == tt, number, comp)
-        part = coef[s, :panel_rows, :]
+        part = coef[h, slot]
         for k in range(COMPS):
             mask = (comp == k).astype(f32).astype(bf16)
             spread_coef[step % 2, k * panel_rows:(k + 1) * panel_rows, :] = part * mask
-        dosage[s, height:, :] = coef[s, panel_rows:, :]
+        note = means[h, slot]
+        average = jnp.concatenate([note[t:t + 1] for t in range(block_tiles)], axis=1)
+        high = average.astype(bf16).astype(f32)
+        rest = average - high
+        middle = rest.astype(bf16).astype(f32)
+        dosage[h, slot, height:, :] = jnp.where(
+            low_wide == 0, high, jnp.where(low_wide == 1, middle, jnp.where(low_wide == 2, rest - middle, 0.0))
+        ).astype(bf16)
         product = lax.dot_general(
-            dosage[s], spread_coef[step % 2], (((1,), (1,)), ((), ())), preferred_element_type=f32
+            dosage[h, slot], spread_coef[step % 2], (((1,), (1,)), ((), ())), preferred_element_type=f32
         )
         if step == 0:
             total[...] = product
@@ -352,12 +457,15 @@
     stacked = jnp.concatenate(sums, axis=0)
     picker = (
         lax.div(lax.broadcasted_iota(jnp.int32, (span, 128), 0), probe_count)
-        == lax.broadcasted_iota(jnp.int32, (span, 128), 1)
+        == lax.rem(lax.broadcasted_iota(jnp.int32, (span, 128), 1), COMPS)
     ).astype(f32)
     pairs = jnp.dot(stacked, picker, precision=HIGHEST, preferred_element_type=f32)
-
-    sum_samp[me, 0:COMPS, :] = pairs
-    sum_samp[me, COMPS:, :] = jnp.broadcast_to(energy, (8, 128))
+    row_id = lax.broadcasted_iota(jnp.int32, (COMPS, 128), 0)
+    lane_id = lax.broadcasted_iota(jnp.int32, (COMPS, 128), 1)
+    flat = jnp.sum(jnp.where(lax.div(lane_id, COMPS) == row_id, pairs, 0.0), axis=0, keepdims=True)
+    flat = flat + pltpu.roll(jnp.broadcast_to(energy, (8, 128)), COMPS * COMPS, 1)[0:1]
+
+    sum_samp[me] = flat
     for o in range(1, n_samp):
         remote(sum_samp.at[me], sum_samp.at[me], send_samp.at[o], recv_samp.at[o], "samp", samp_peer(o)).start()
     for o in range(1, n_samp):
@@ -376,24 +484,35 @@
     everything = sum_snp[0]
     for i in range(1, n_snp):
         everything = everything + sum_snp[i]
-    row_id = lax.broadcasted_iota(jnp.int32, (COMPS, 128), 0)
-    lane_id = lax.broadcasted_iota(jnp.int32, (COMPS, 128), 1)
-    turn = (row_id - lane_id) & (COMPS - 1)
-    trace = jnp.zeros((COMPS, 128), f32)
-    for d in range(COMPS):
-        trace = jnp.where(turn == d, everything[d:d + 1], trace)
+    column_id = lax.rem(lane_id, COMPS)
+    keep_lane = (lane_id < COMPS * COMPS) & (lax.div(lane_id, COMPS) == ((row_id - column_id) & (COMPS - 1)))
+    chosen = jnp.where(keep_lane, jnp.broadcast_to(everything, (COMPS, 128)), 0.0)
+    fold = (
+        lax.rem(lax.broadcasted_iota(jnp.int32, (128, 128), 0), COMPS)
+        == lax.broadcasted_iota(jnp.int32, (128, 128), 1)
+    ).astype(f32)
+    trace = jnp.dot(chosen, fold, precision=HIGHEST, preferred_element_type=f32)
     trace = trace * (SNPS / (COMPS * probe_count)) / (weight_total * weight_total)
     traces_ref[...] = trace[:, :COMPS]
-    yky_ref[...] = (everything[COMPS:COMPS + 1] / weight_total)[:, :COMPS]
-
+    energies = pltpu.roll(jnp.broadcast_to(everything, (8, 128)), 128 - COMPS * COMPS, 1)[0:1]
+    yky_ref[...] = (energies / weight_total)[:, :COMPS]
+
+    sent = []
+    for h in range(halves):
+        for o in range(n_line):
+            sent += pair_copies(h, o)
+        for o in range(1, n_line):
+            sent += line_copies(h, o)
+            sent += coef_copies(h, 0, (n_line - o) * PAIR, o, line_peer(o))
+            sent += coef_copies(h, o * PAIR, o * PAIR + 1, n_line + o, partner)
+        sent += coef_copies(h, 0, 1, 0, partner)
     for o in range(1, n_samp):
-        remote(panel_out.at[o], panel_in.at[o], send_panel.at[o], recv_panel.at[o], "samp", samp_peer(o)).wait_send()
-        remote(moment_out.at[o], moment_in.at[o], send_moment.at[o], recv_moment.at[o], "samp", samp_peer(o)).wait_send()
-        remote(coef.at[0], coef.at[n_samp - o], send_coef.at[o], recv_coef.at[n_samp - o], "samp", samp_peer(o)).wait_send()
-        remote(sum_samp.at[me], sum_samp.at[me], send_samp.at[o], recv_samp.at[o], "samp", samp_peer(o)).wait_send()
+        sent.append(remote(sum_samp.at[me], sum_samp.at[me], send_samp.at[o], recv_samp.at[o], "samp", samp_peer(o)))
     for o in range(1, n_snp):
-        remote(piece_out.at[o], piece_in.at[o], send_piece.at[o], recv_piece.at[o], "snp", snp_peer(o)).wait_send()
-        remote(sum_mid, sum_snp.at[mine], send_snp.at[o], recv_snp.at[o], "snp", snp_peer(o)).wait_send()
+        sent.append(remote(piece_out.at[o], piece_in.at[o], send_piece.at[o], recv_piece.at[o], "snp", snp_peer(o)))
+        sent.append(remote(sum_mid, sum_snp.at[mine], send_snp.at[o], recv_snp.at[o], "snp", snp_peer(o)))
+    for item in sent:
+        item.wait_send()
 
 
 def on_device_fused(geno_words, counts, probes, phenotype, tile_comp):
@@ -401,7 +520,11 @@
     height = geno_words.shape[0]
     tiles_local = geno_words.shape[1] * 16 // 128
     probe_count = probes.shape[1]
-    width = tiles_local // n_samp * 128
+    n_line = n_samp // PAIR
+    halves = HALVES if tiles_local // n_samp % HALVES == 0 else 1
+    block_tiles = tiles_local // n_samp // halves
+    width = block_tiles * 128
+    note_rows = -(-(3 * block_tiles + 1) // 8) * 8
     span = COMPS * probe_count
     rows = height // n_snp
     f32, bf16 = jnp.float32, jnp.bfloat16
@@ -409,7 +532,7 @@
     smem = pl.BlockSpec(memory_space=pltpu.SMEM)
     dma = pltpu.SemaphoreType.DMA
     images, traces, yky = pl.pallas_call(
-        functools.partial(whole_kernel, (n_samp, n_snp, tiles_local, probe_count)),
+        functools.partial(whole_kernel, (n_samp, n_snp, tiles_local, probe_count, halves)),
         out_shape=(
             jax.ShapeDtypeStruct((rows, span), bf16),
             jax.ShapeDtypeStruct((COMPS, COMPS), f32),
@@ -418,38 +541,37 @@
         in_specs=[smem] + [vmem] * 5,
         out_specs=(vmem, vmem, vmem),
         scratch_shapes=[
-            pltpu.VMEM((n_samp, height + 16, width), bf16),
-            pltpu.VMEM((n_samp, probe_count, width), bf16),
-            pltpu.VMEM((n_samp, 8, width), f32),
-            pltpu.VMEM((n_samp, probe_count, width), bf16),
-            pltpu.VMEM((n_samp, 8, width), f32),
-            pltpu.VMEM((n_samp, probe_count + 16, width), bf16),
+            pltpu.VMEM((halves, n_samp, height + 16, width), bf16),
+            pltpu.VMEM((halves, n_line, probe_count, width), f32),
+            pltpu.VMEM((halves, n_line, probe_count, width), bf16),
+            pltpu.VMEM((halves, n_line, note_rows, 128), f32),
+            pltpu.VMEM((halves, n_line, probe_count, width), bf16),
+            pltpu.VMEM((halves, n_line, note_rows, 128), f32),
+            pltpu.VMEM((halves, n_line, probe_count, width), bf16),
+            pltpu.VMEM((halves, n_line, note_rows, 128), f32),
+            pltpu.VMEM((halves, n_line, probe_count, width), bf16),
+            pltpu.VMEM((halves, n_line, note_rows, 128), f32),
+            pltpu.VMEM((halves, n_samp, probe_count, width), bf16),
+            pltpu.VMEM((halves, n_samp, 8, 128), f32),
             pltpu.VMEM((2, span, width), bf16),
             pltpu.VMEM((height + 16, span), f32),
             pltpu.VMEM((n_snp, rows, span), bf16),
             pltpu.VMEM((n_snp, rows, span), bf16),
-            pltpu.VMEM((n_samp, COMPS + 8, 128), f32),
-            pltpu.VMEM((n_snp, COMPS + 8, 128), f32),
-            pltpu.VMEM((COMPS + 8, 128), f32),
-            dma((n_samp,)),
-            dma((n_samp,)),
-            dma((n_samp,)),
-            dma((n_samp,)),
-            dma((n_samp,)),
-            dma((n_samp,)),
-            dma((n_snp,)),
-            dma((n_snp,)),
-            dma((n_samp,)),
-            dma((n_samp,)),
-            dma((n_snp,)),
-            dma((n_snp,)),
-        ],
+            pltpu.VMEM((n_samp, 1, 128), f32),
+            pltpu.VMEM((n_snp, 1, 128), f32),
+            pltpu.VMEM((1, 128), f32),
+        ]
+        + [dma((halves, n_line))] * 8
+        + [dma((halves, n_samp))] * 4
+        + [dma((n_snp,))] * 2
+        + [dma((n_samp,))] * 2
+        + [dma((n_snp,))] * 2,
         compiler_params=pltpu.CompilerParams(collective_id=0, has_side_effects=True),
     )(
         tile_comp,
         geno_words,
         counts.reshape(1, -1),
-        probes,
+        probes.T,
         phenotype.reshape(1, -1),
         tile_comp.reshape(1, -1),
     )
@@ -459,7 +581,7 @@
 def dispatch(geno_words, counts, probes, phenotype, tile_comp):
     n_samp, n_snp = lax.axis_size("samp"), lax.axis_size("snp")
     tiles_local = geno_words.shape[1] * 16 // 128
-    whole_tiles = tiles_local % n_samp == 0 and tile_comp.shape[0] == 128
+    whole_tiles = tiles_local % n_samp == 0 and n_samp % PAIR == 0 and tile_comp.shape[0] == 128
     whole_rows = geno_words.shape[0] % (16 * n_snp) == 0 and probes.shape[1] == 64
     body = on_device_fused if whole_tiles and whole_rows else on_device
     return body(geno_words, counts, probes, phenotype, tile_comp)

time: 58.9 us -> 43.2 us (0.73)
  Pallas kernels: 53.9 us -> 39.8 us
  local copies, waits for them, and re-layouts: 4.08 us -> 2.59 us
    pallas_call x1, Pallas kernels: 53.9 us -> 39.8 us  [on_device_fused(): pl.pallas_call(functools.partial(whole_kernel, (n_samp, n_snp, tiles_loca...]
    unnamed x8 -> x7, local copies, waits for them, and re-layouts: 4.08 us -> 2.59 us
where the time goes in v2:
time: 43.2 us; the launch traced here: 43 us
  Pallas kernels  39.8 us (92%)
  local copies, waits for them, and re-layouts  2.59 us (6%)
  between operations  0.65 us (2%)
    pallas_call x1, Pallas kernels, on_device_fused(): pl.pallas_call(functools.partial(whole_kernel, (n_samp, n_snp, tiles_loca...  39.8 us
    unnamed x7, local copies, waits for them, and re-layouts  2.59 us

profile of v2, /device:TPU:0, one launch (start us, length us, event | category | flops | bytes accessed | tf_op | source)
XLA Modules:
  0.0 43.0 jit_solution(2016978119682237217)
XLA Ops:
  0.6 39.8 %shard_map.76 = (bf16[64,512]{1,0:T(8,128)(2,1)}, f32[8,8]{1,0:T(8,128)}, f32[1,8]{1,0:T(1,128)}) custom-call(s32[128]{0:T(128)} %tile_smem.1, s32[256,256]{1,0:T(8,128)} %words_ref.1, s32[1,256]{1,0:T(1,128)} %bitcast.7, bf16[64,256]{1,0:T(8,128)(2,1)} %bitcast.5, f32[1,256]{1,0:T(1,128)} %bitcast.8, s32[1,128]{1,0:T(1,128)} %bitcast.6), custom_call_target="tpu_custom_call" | custom-call | tf_op jit(solution)/shard_map/pallas_call | solution.py:534
  40.4 0.0 copy-start
  40.4 1.5 %copy.11 = bf16[64,512]{1,0:T(8,128)(2,1)} copy(bf16[64,512]{1,0:T(8,128)(2,1)} %get-tuple-element.12) | data formatting | bytes 131072
  41.9 0.0 copy-done
  41.9 0.0 copy-start.1
  41.9 0.6 %copy.12 = f32[8,8]{1,0:T(8,128)} copy(f32[8,8]{1,0:T(8,128)S(1)} %copy-done) | data formatting | bytes 512
  42.5 0.0 copy-done.1
  42.5 0.5 %copy.13 = f32[8]{0:T(128)} copy(f32[8]{0:T(128)S(1)} %bitcast.9) | data formatting | bytes 64
Async XLA Ops:
  40.4 1.5 %copy-start = (f32[8,8]{1,0:T(8,128)S(1)}, f32[8,8]{1,0:T(8,128)}, u32[]{:S(2)}) copy-start(f32[8,8]{1,0:T(8,128)} %get-tuple-element.13) | copy-start | bytes 772
  41.9 0.6 %copy-start.1 = (f32[1,8]{1,0:T(1,128)S(1)}, f32[1,8]{1,0:T(1,128)}, u32[]{:S(2)}) copy-start(f32[1,8]{1,0:T(1,128)} %get-tuple-element.8) | copy-start | bytes 100

commit v3 on v2

--- a/solution.py
+++ b/solution.py
@@ -138,9 +138,7 @@
     total,
     piece_out,
     piece_in,
-    sum_samp,
-    sum_snp,
-    sum_mid,
+    sum_all,
     send_pair,
     recv_pair,
     send_pair_note,
@@ -155,10 +153,8 @@
     recv_means,
     send_piece,
     recv_piece,
-    send_samp,
-    recv_samp,
-    send_snp,
-    recv_snp,
+    send_all,
+    recv_all,
 ):
     n_samp, n_snp, tiles_local, probe_count, halves = sizes
     me, mine = lax.axis_index("samp"), lax.axis_index("snp")
@@ -180,20 +176,41 @@
     def snp_peer(offset):
         return lax.rem(mine + offset, n_snp)
 
+    def across(offset):
+        place, bit = line, 1
+        while bit <= offset:
+            if offset & bit:
+                place = place + bit - 2 * bit * lax.rem(lax.div(line, bit), 2)
+            bit = 2 * bit
+        return place
+
     def line_peer(offset):
-        return lax.rem(line + offset, n_line) * PAIR + side
+        return across(offset) * PAIR + side
 
     def owner_of(offset, other):
-        return lax.rem(line + offset, n_line) * PAIR + (1 - side if other else side)
-
-    far_first = sorted(range(1, n_line), key=lambda o: -min(o, n_line - o))
-    near_first = sorted(range(1, n_line), key=lambda o: min(o, n_line - o))
+        return across(offset) * PAIR + (1 - side if other else side)
+
+    half_line = n_line // 2
+    far_first = list(range(half_line, n_line)) + list(range(1, half_line))
+    near_first = list(range(1, half_line)) + list(reversed(range(half_line, n_line)))
+
+    everyone = n_samp * n_snp
+    spot = me * n_snp + mine
+
+    def anyone(offset):
+        other = lax.rem(spot + offset, everyone)
+        return {"samp": lax.div(other, n_snp), "snp": lax.rem(other, n_snp)}
 
     barrier = pltpu.get_barrier_semaphore()
-    for o in range(1, n_samp):
-        pl.semaphore_signal(barrier, inc=1, device_id={"samp": samp_peer(o)}, device_id_type=MESH)
-    for o in range(1, n_snp):
-        pl.semaphore_signal(barrier, inc=1, device_id={"snp": snp_peer(o)}, device_id_type=MESH)
+    for o in range(1, everyone):
+        pl.semaphore_signal(barrier, inc=1, device_id=anyone(o), device_id_type=MESH)
+
+    def sum_copy(slot, offset):
+        return pltpu.make_async_remote_copy(
+            src_ref=sum_all.at[slot], dst_ref=sum_all.at[slot],
+            send_sem=send_all.at[offset], recv_sem=recv_all.at[offset],
+            device_id=anyone(offset), device_id_type=MESH,
+        )
 
     def remote(src, dst, send, recv, axis, peer):
         return pltpu.make_async_remote_copy(
@@ -291,7 +308,7 @@
             pair_out[h, o] = panel.astype(bf16)
             pair_note_out[h, o] = note_of(first, square, cross, own_row)
             if not waited:
-                pl.semaphore_wait(barrier, n_samp + n_snp - 2)
+                pl.semaphore_wait(barrier, everyone - 1)
                 waited = True
             start(pair_copies(h, o))
     own_notes = {}
@@ -385,7 +402,7 @@
             axis=0,
         )
         for o in far_first:
-            start(coef_copies(h, 0, (n_line - o) * PAIR, o, line_peer(o)))
+            start(coef_copies(h, 0, o * PAIR, o, line_peer(o)))
         start(coef_copies(h, 0, 1, 0, partner))
         energy_snps = pheno_unit * pheno_unit * inverse
         for t in range(block_tiles):
@@ -465,25 +482,12 @@
     flat = jnp.sum(jnp.where(lax.div(lane_id, COMPS) == row_id, pairs, 0.0), axis=0, keepdims=True)
     flat = flat + pltpu.roll(jnp.broadcast_to(energy, (8, 128)), COMPS * COMPS, 1)[0:1]
 
-    sum_samp[me] = flat
-    for o in range(1, n_samp):
-        remote(sum_samp.at[me], sum_samp.at[me], send_samp.at[o], recv_samp.at[o], "samp", samp_peer(o)).start()
-    for o in range(1, n_samp):
-        source = lax.rem(me + n_samp - o, n_samp)
-        remote(sum_samp.at[source], sum_samp.at[source], send_samp.at[o], recv_samp.at[o], "samp", samp_peer(o)).wait_recv()
-    group_sum = sum_samp[0]
-    for i in range(1, n_samp):
-        group_sum = group_sum + sum_samp[i]
-    sum_mid[...] = group_sum
-    for o in range(1, n_snp):
-        remote(sum_mid, sum_snp.at[mine], send_snp.at[o], recv_snp.at[o], "snp", snp_peer(o)).start()
-    sum_snp[mine] = group_sum
-    for o in range(1, n_snp):
-        source = lax.rem(mine + n_snp - o, n_snp)
-        remote(sum_mid, sum_snp.at[source], send_snp.at[o], recv_snp.at[o], "snp", snp_peer(o)).wait_recv()
-    everything = sum_snp[0]
-    for i in range(1, n_snp):
-        everything = everything + sum_snp[i]
+    sum_all[spot] = flat
+    for o in range(1, everyone):
+        sum_copy(spot, o).start()
+    for o in range(1, everyone):
+        sum_copy(lax.rem(spot + everyone - o, everyone), o).wait_recv()
+    everything = jnp.sum(sum_all[...], axis=0)
     column_id = lax.rem(lane_id, COMPS)
     keep_lane = (lane_id < COMPS * COMPS) & (lax.div(lane_id, COMPS) == ((row_id - column_id) & (COMPS - 1)))
     chosen = jnp.where(keep_lane, jnp.broadcast_to(everything, (COMPS, 128)), 0.0)
@@ -503,16 +507,21 @@
             sent += pair_copies(h, o)
         for o in range(1, n_line):
             sent += line_copies(h, o)
-            sent += coef_copies(h, 0, (n_line - o) * PAIR, o, line_peer(o))
+            sent += coef_copies(h, 0, o * PAIR, o, line_peer(o))
             sent += coef_copies(h, o * PAIR, o * PAIR + 1, n_line + o, partner)
         sent += coef_copies(h, 0, 1, 0, partner)
-    for o in range(1, n_samp):
-        sent.append(remote(sum_samp.at[me], sum_samp.at[me], send_samp.at[o], recv_samp.at[o], "samp", samp_peer(o)))
+    for o in range(1, everyone):
+        sent.append(sum_copy(spot, o))
     for o in range(1, n_snp):
         sent.append(remote(piece_out.at[o], piece_in.at[o], send_piece.at[o], recv_piece.at[o], "snp", snp_peer(o)))
-        sent.append(remote(sum_mid, sum_snp.at[mine], send_snp.at[o], recv_snp.at[o], "snp", snp_peer(o)))
     for item in sent:
         item.wait_send()
+
+
+def hand_over(images_in, traces_in, yky_in, images_ref, traces_ref, yky_ref):
+    images_ref[...] = images_in[...]
+    traces_ref[...] = traces_in[...]
+    yky_ref[...] = yky_in[...]
 
 
 def on_device_fused(geno_words, counts, probes, phenotype, tile_comp):
@@ -557,15 +566,12 @@
             pltpu.VMEM((height + 16, span), f32),
             pltpu.VMEM((n_snp, rows, span), bf16),
             pltpu.VMEM((n_snp, rows, span), bf16),
-            pltpu.VMEM((n_samp, 1, 128), f32),
-            pltpu.VMEM((n_snp, 1, 128), f32),
-            pltpu.VMEM((1, 128), f32),
+            pltpu.VMEM((n_samp * n_snp, 1, 128), f32),
         ]
         + [dma((halves, n_line))] * 8
         + [dma((halves, n_samp))] * 4
         + [dma((n_snp,))] * 2
-        + [dma((n_samp,))] * 2
-        + [dma((n_snp,))] * 2,
+        + [dma((n_samp * n_snp,))] * 2,
         compiler_params=pltpu.CompilerParams(collective_id=0, has_side_effects=True),
     )(
         tile_comp,
@@ -575,13 +581,19 @@
         phenotype.reshape(1, -1),
         tile_comp.reshape(1, -1),
     )
+    images, traces, yky = pl.pallas_call(
+        hand_over,
+        out_shape=tuple(jax.ShapeDtypeStruct(v.shape, v.dtype) for v in (images, traces, yky)),
+        in_specs=[vmem] * 3,
+        out_specs=(vmem, vmem, vmem),
+    )(images, traces, yky)
     return (images, traces, yky.reshape(-1))
 
 
 def dispatch(geno_words, counts, probes, phenotype, tile_comp):
     n_samp, n_snp = lax.axis_size("samp"), lax.axis_size("snp")
     tiles_local = geno_words.shape[1] * 16 // 128
-    whole_tiles = tiles_local % n_samp == 0 and n_samp % PAIR == 0 and tile_comp.shape[0] == 128
+    whole_tiles = tiles_local % n_samp == 0 and n_samp % PAIR == 0 and (n_samp // PAIR) & (n_samp // PAIR - 1) == 0 and tile_comp.shape[0] == 128
     whole_rows = geno_words.shape[0] % (16 * n_snp) == 0 and probes.shape[1] == 64
     body = on_device_fused if whole_tiles and whole_rows else on_device
     return body(geno_words, counts, probes, phenotype, tile_comp)

time: 43.2 us -> 41 us (0.949)
  local copies, waits for them, and re-layouts: 2.59 us -> 0 us
    unnamed x7 -> x0, local copies, waits for them, and re-layouts: 2.59 us -> none
    pallas_call x0 -> x1, Pallas kernels: none -> 1.48 us  [on_device_fused(): pl.pallas_call(hand_over, out_shape=tuple((jax.ShapeDtypeStruct(v.shape,...]
    pallas_call x1, Pallas kernels: 39.8 us -> 38.7 us  [on_device_fused(): pl.pallas_call(functools.partial(whole_kernel, (n_samp, n_snp, tiles_loca...]
where the time goes in v3:
time: 41 us; the launch traced here: 40.8 us
  Pallas kernels  40.2 us (98%)
  between operations  0.64 us (2%)
    pallas_call x1, Pallas kernels, on_device_fused(): pl.pallas_call(functools.partial(whole_kernel, (n_samp, n_snp, tiles_loca...  38.7 us
    pallas_call x1, Pallas kernels, on_device_fused(): pl.pallas_call(hand_over, out_shape=tuple((jax.ShapeDtypeStruct(v.shape,...  1.48 us

profile of v3, /device:TPU:0, one launch (start us, length us, event | category | flops | bytes accessed | tf_op | source)
XLA Modules:
  0.0 40.8 jit_solution(9906078281080887132)
XLA Ops:
  0.6 38.7 %shard_map.76 = (bf16[64,512]{1,0:T(8,128)(2,1)}, f32[8,8]{1,0:T(8,128)}, f32[1,8]{1,0:T(1,128)}) custom-call(s32[128]{0:T(128)} %tile_smem.1, s32[256,256]{1,0:T(8,128)} %words_ref.1, s32[1,256]{1,0:T(1,128)} %bitcast.7, bf16[64,256]{1,0:T(8,128)(2,1)} %bitcast.5, f32[1,256]{1,0:T(1,128)} %bitcast.8, s32[1,128]{1,0:T(1,128)} %bitcast.6), custom_call_target="tpu_custom_call" | custom-call | tf_op jit(solution)/shard_map/pallas_call | solution.py:543
  39.3 1.5 %shard_map.77 = (bf16[64,512]{1,0:T(8,128)(2,1)}, f32[8,8]{1,0:T(8,128)}, f32[1,8]{1,0:T(1,128)}) custom-call(bf16[64,512]{1,0:T(8,128)(2,1)} %get-tuple-element.9.images_in, f32[8,8]{1,0:T(8,128)} %get-tuple-element.10.traces_in, f32[1,8]{1,0:T(1,128)} %get-tuple-element.11.yky_in), custom_call_target="tpu_custom_call" | custom-call | tf_op jit(solution)/shard_map/pallas_call | solution.py:584
